TPU v7x, 256 devices: a 2x2x32 block of a 4x8x32 slice. The times are simulated.
256 devices in a mesh: groups: 4 (over y, x), ctx: 32 (over z), tp: 2 (over core).
Axes of the slice: x: 2, y: 2, z: 32, core: 2. Of those that a mesh axis runs over, the one named last changes fastest.
The devices are a block of a 4x8x32 slice.
Arguments:
- query_states: bfloat16 [32768, 32, 128], P(('groups', 'ctx'), 'tp'), parts along dimension 0, may hold values from -8 to 8
- key_states: bfloat16 [32768, 4, 128], P(('groups', 'ctx'), 'tp'), parts along dimension 0, may hold values from -8 to 8
- value_rows: bfloat16 [32768, 4, 128], P(('groups', 'ctx'), 'tp'), parts along dimension 0, may hold values from -12 to 12
- positions: int32 [32768], P(('groups', 'ctx')), parts along dimension 0, may hold values from 0 to 8191, as said below
- out_weight: bfloat16 [4096, 4096], P('tp', 'ctx'), may hold values from -0.375 to 0.375
Outputs:
- projected: bfloat16 [32768, 4096], P(('groups', 'ctx'), 'tp'), parts along dimension 0
There are 4 independent parts, one for each index of `groups`. A program takes and returns all parts, laid end to end along the dimension named above; an argument that names none is the same for every part. Nothing has to cross between parts.
Inputs may be any that keep to these rules, and one draw needn't show every extreme that they name: Each of 0 to 8191 appears once. Half-block b holds positions b * 128 to (b + 1) * 128 - 1. The 256 rows of one device along ctx hold half-block j and then half-block 64 - 1 - j, each in rising order, for a j below 32 that differs from device to device.
All inputs are finite; a program needn't handle non-finite values.
Results may differ from a plain program's by a relative error of at most 0.01.
Values may be sent and summed in bfloat16 or wider, within the bound.
A program may use at most 64 MiB of HBM per device.

v0:
```python
import jax
import jax.numpy as jnp
from jax import lax
from jax.sharding import PartitionSpec as P

LOW_START = -1e30


def for_sending(value):
    return jax.tree.map(lambda a: a.astype(jnp.bfloat16) if a.dtype == jnp.float32 else a, value)


def from_behind(value, axis, by):
    devices = lax.axis_size(axis)
    return lax.ppermute(value, axis, [(i, (i + by) % devices) for i in range(devices)])


def cut_along(value, dim, devices):
    before, after = (value.shape[:dim], value.shape[dim + 1 :])
    return jnp.moveaxis(value.reshape(*before, devices, -1, *after), dim, 0)


def sent_and_summed(value, axis, dim):
    parts = cut_along(value, dim, lax.axis_size(axis))
    arrived = lax.all_to_all(parts, axis, split_axis=0, concat_axis=0, tiled=True)
    return arrived.astype(jnp.float32).sum(axis=0)


def attend_block(partial_state, query_part, key_part, value_part, visible):
    largest, denominator, numerator = partial_state
    scores = jnp.einsum("qkgd,skd->kgqs", query_part, key_part, preferred_element_type=jnp.float32)
    scores = scores * query_part.shape[-1] ** (-0.5)
    if visible is not None:
        scores = jnp.where(visible[None, None], scores, -jnp.inf)
    new_max = jnp.maximum(largest, jnp.max(scores, axis=-1))
    factor = jnp.exp(largest - new_max)
    exp_scores = jnp.exp(scores - new_max[..., None])
    denominator = denominator * factor + jnp.sum(exp_scores, axis=-1)
    weighted = jnp.einsum(
        "kgqs,skd->kgqd",
        exp_scores.astype(jnp.bfloat16),
        value_part,
        preferred_element_type=jnp.float32,
    )
    return (new_max, denominator, numerator * factor[..., None] + weighted)


def update_half(partial_state, grouped, offset, key_part, value_part):
    span_rows = key_part.shape[0]
    sliced = tuple(
        (lax.dynamic_slice_in_dim(member, offset, span_rows, 2) for member in partial_state)
    )
    query_part = lax.dynamic_slice_in_dim(grouped, offset, span_rows, 0)
    renewed = attend_block(sliced, query_part, key_part, value_part, None)
    return tuple(
        (
            lax.dynamic_update_slice_in_dim(member, updated, offset, 2)
            for member, updated in zip(partial_state, renewed)
        )
    )


def remote_step(partial_state, grouped, own_first, arrived):
    key_part, value_part, key_places = arrived
    half_rows = key_part.shape[0] // 2
    partial_state = update_half(
        partial_state, grouped, half_rows, key_part[:half_rows], value_part[:half_rows]
    )
    offset = jnp.where(key_places[0] < own_first, 0, half_rows).astype(jnp.int32)
    key_pick = lax.dynamic_slice_in_dim(key_part, offset, half_rows, 0)
    value_pick = lax.dynamic_slice_in_dim(value_part, offset, half_rows, 0)
    return update_half(partial_state, grouped, offset, key_pick, value_pick)


def local(query_states, key_states, value_rows, positions, out_weight):
    tokens, query_heads, head_size = query_states.shape
    kv_heads = key_states.shape[1]
    grouped = query_states.reshape(tokens, kv_heads, query_heads // kv_heads, head_size)
    row_shape = (kv_heads, query_heads // kv_heads, tokens)
    partial_state = (
        jnp.full(row_shape, LOW_START, jnp.float32),
        jnp.zeros(row_shape, jnp.float32),
        jnp.zeros(row_shape + (head_size,), jnp.float32),
    )
    visible = positions[None, :] <= positions[:, None]
    partial_state = attend_block(partial_state, grouped, key_states, value_rows, visible)
    own_first = positions[0]
    own_block = (key_states, value_rows, positions)

    def forward_turn(number, status):
        arrived = from_behind(for_sending(status[0]), "ctx", 1)
        return (arrived, remote_step(status[1], grouped, own_first, arrived))

    partial_state = lax.fori_loop(
        0, lax.axis_size("ctx") - 1, forward_turn, (own_block, partial_state)
    )[1]
    largest, denominator, numerator = partial_state
    attended = numerator / denominator[..., None]
    attended = (
        jnp.transpose(attended, (2, 0, 1, 3))
        .reshape(tokens, query_heads * head_size)
        .astype(jnp.bfloat16)
    )
    combined = jnp.dot(
        attended,
        lax.all_gather(out_weight, "ctx", axis=1, tiled=True),
        preferred_element_type=jnp.float32,
    )
    return sent_and_summed(combined.astype(jnp.bfloat16), "tp", 1).astype(jnp.bfloat16)


def solution(mesh):
    in_specs = (
        P(("groups", "ctx"), "tp", None),
        P(("groups", "ctx"), "tp", None),
        P(("groups", "ctx"), "tp", None),
        P(("groups", "ctx")),
        P("tp", "ctx"),
    )
    out_specs = P(("groups", "ctx"), "tp")
    return jax.shard_map(local, mesh=mesh, in_specs=in_specs, out_specs=out_specs, check_vma=False)
```

profile of v0, /device:TPU:37, one launch (start us, length us, event | category | flops | bytes accessed | tf_op | source)
XLA Modules:
  0.0 504.3 jit_solution(16106959090836966617)
XLA Ops:
  16.2 3.3 fusion.29
  19.4 436.8 %while.20 = (s32[]{:T(128)}, bf16[256,2,128]{2,0,1:T(8,128)(2,1)}, bf16[256,2,128]{2,0,1:T(8,128)(2,1)}, s32[256]{0:T(256)S(1)}, f32[2,8,256]{2,1,0:T(8,128)S(1)...) while((s32[]{:T(128)}, bf16[256,2,128]{2,0,1:T(8,128)(2,1)}, ...), condition=%wide.region_7.8_spmd, body=%wide.region_2.7_spmd.sunk | while | flops 272637952 | bytes 13689107 | solution.py:94
  25.9 20.7 %collective-permute-done.2 = s32[256]{0:T(256)S(1)} collective-permute-done((s32[256]{0:T(256)S(1)}, s32[256]{0:T(256)S(1)}, u32[]{:S(2)}, u32[]{:S(2)}) %collective-permute-start.2) | collective-permute-done | bytes 1056 | tf_op jit(solution)/shard_map/while/body/eval_jaxpr/ppermute | solution.py:15
  52.6 5.0 collective-permute-done.2
  63.4 5.4 %collective-permute-done.2 = s32[256]{0:T(256)S(1)} collective-permute-done((s32[256]{0:T(256)S(1)}, s32[256]{0:T(256)S(1)}, u32[]{:S(2)}, u32[]{:S(2)}) %collective-permute-start.2) | collective-permute-done | bytes 1056 | tf_op jit(solution)/shard_map/while/body/eval_jaxpr/ppermute | solution.py:15
  74.7 7.8 %collective-permute-done.2 = s32[256]{0:T(256)S(1)} collective-permute-done((s32[256]{0:T(256)S(1)}, s32[256]{0:T(256)S(1)}, u32[]{:S(2)}, u32[]{:S(2)}) %collective-permute-start.2) | collective-permute-done | bytes 1056 | tf_op jit(solution)/shard_map/while/body/eval_jaxpr/ppermute | solution.py:15
  89.2 8.4 %collective-permute-done.2 = s32[256]{0:T(256)S(1)} collective-permute-done((s32[256]{0:T(256)S(1)}, s32[256]{0:T(256)S(1)}, u32[]{:S(2)}, u32[]{:S(2)}) %collective-permute-start.2) | collective-permute-done | bytes 1056 | tf_op jit(solution)/shard_map/while/body/eval_jaxpr/ppermute | solution.py:15
  103.4 7.8 %collective-permute-done.2 = s32[256]{0:T(256)S(1)} collective-permute-done((s32[256]{0:T(256)S(1)}, s32[256]{0:T(256)S(1)}, u32[]{:S(2)}, u32[]{:S(2)}) %collective-permute-start.2) | collective-permute-done | bytes 1056 | tf_op jit(solution)/shard_map/while/body/eval_jaxpr/ppermute | solution.py:15
  117.0 8.8 %collective-permute-done.2 = s32[256]{0:T(256)S(1)} collective-permute-done((s32[256]{0:T(256)S(1)}, s32[256]{0:T(256)S(1)}, u32[]{:S(2)}, u32[]{:S(2)}) %collective-permute-start.2) | collective-permute-done | bytes 1056 | tf_op jit(solution)/shard_map/while/body/eval_jaxpr/ppermute | solution.py:15
  131.8 9.4 %collective-permute-done.2 = s32[256]{0:T(256)S(1)} collective-permute-done((s32[256]{0:T(256)S(1)}, s32[256]{0:T(256)S(1)}, u32[]{:S(2)}, u32[]{:S(2)}) %collective-permute-start.2) | collective-permute-done | bytes 1056 | tf_op jit(solution)/shard_map/while/body/eval_jaxpr/ppermute | solution.py:15
  147.0 9.6 %collective-permute-done.2 = s32[256]{0:T(256)S(1)} collective-permute-done((s32[256]{0:T(256)S(1)}, s32[256]{0:T(256)S(1)}, u32[]{:S(2)}, u32[]{:S(2)}) %collective-permute-start.2) | collective-permute-done | bytes 1056 | tf_op jit(solution)/shard_map/while/body/eval_jaxpr/ppermute | solution.py:15
  162.4 9.3 %collective-permute-done.2 = s32[256]{0:T(256)S(1)} collective-permute-done((s32[256]{0:T(256)S(1)}, s32[256]{0:T(256)S(1)}, u32[]{:S(2)}, u32[]{:S(2)}) %collective-permute-start.2) | collective-permute-done | bytes 1056 | tf_op jit(solution)/shard_map/while/body/eval_jaxpr/ppermute | solution.py:15
  178.4 9.6 %collective-permute-done.2 = s32[256]{0:T(256)S(1)} collective-permute-done((s32[256]{0:T(256)S(1)}, s32[256]{0:T(256)S(1)}, u32[]{:S(2)}, u32[]{:S(2)}) %collective-permute-start.2) | collective-permute-done | bytes 1056 | tf_op jit(solution)/shard_map/while/body/eval_jaxpr/ppermute | solution.py:15
  195.0 8.2 %collective-permute-done.2 = s32[256]{0:T(256)S(1)} collective-permute-done((s32[256]{0:T(256)S(1)}, s32[256]{0:T(256)S(1)}, u32[]{:S(2)}, u32[]{:S(2)}) %collective-permute-start.2) | collective-permute-done | bytes 1056 | tf_op jit(solution)/shard_map/while/body/eval_jaxpr/ppermute | solution.py:15
  209.3 6.7 %collective-permute-done.2 = s32[256]{0:T(256)S(1)} collective-permute-done((s32[256]{0:T(256)S(1)}, s32[256]{0:T(256)S(1)}, u32[]{:S(2)}, u32[]{:S(2)}) %collective-permute-start.2) | collective-permute-done | bytes 1056 | tf_op jit(solution)/shard_map/while/body/eval_jaxpr/ppermute | solution.py:15
  224.4 6.6 %collective-permute-done.2 = s32[256]{0:T(256)S(1)} collective-permute-done((s32[256]{0:T(256)S(1)}, s32[256]{0:T(256)S(1)}, u32[]{:S(2)}, u32[]{:S(2)}) %collective-permute-start.2) | collective-permute-done | bytes 1056 | tf_op jit(solution)/shard_map/while/body/eval_jaxpr/ppermute | solution.py:15
  238.9 5.8 %collective-permute-done.2 = s32[256]{0:T(256)S(1)} collective-permute-done((s32[256]{0:T(256)S(1)}, s32[256]{0:T(256)S(1)}, u32[]{:S(2)}, u32[]{:S(2)}) %collective-permute-start.2) | collective-permute-done | bytes 1056 | tf_op jit(solution)/shard_map/while/body/eval_jaxpr/ppermute | solution.py:15
  253.3 6.0 %collective-permute-done.2 = s32[256]{0:T(256)S(1)} collective-permute-done((s32[256]{0:T(256)S(1)}, s32[256]{0:T(256)S(1)}, u32[]{:S(2)}, u32[]{:S(2)}) %collective-permute-start.2) | collective-permute-done | bytes 1056 | tf_op jit(solution)/shard_map/while/body/eval_jaxpr/ppermute | solution.py:15
  267.2 6.2 %collective-permute-done.2 = s32[256]{0:T(256)S(1)} collective-permute-done((s32[256]{0:T(256)S(1)}, s32[256]{0:T(256)S(1)}, u32[]{:S(2)}, u32[]{:S(2)}) %collective-permute-start.2) | collective-permute-done | bytes 1056 | tf_op jit(solution)/shard_map/while/body/eval_jaxpr/ppermute | solution.py:15
  282.4 3.1 collective-permute-done.2
  296.3 3.4 collective-permute-done.2
  310.6 3.4 collective-permute-done.2
  324.9 2.8 collective-permute-done.2
  338.4 4.3 collective-permute-done.2
  386.5 3.4 collective-permute-done.2
  397.6 4.5 collective-permute-done.2
  410.1 3.8 collective-permute-done.2
  422.1 3.9 collective-permute-done.2
  434.3 4.1 collective-permute-done.2
  446.5 4.3 collective-permute-done.2
  459.9 8.4 %convolution_convert_fusion = bf16[256,4096]{1,0:T(8,128)(2,1)S(1)} fusion(bf16[256,2048]{0,1:T(8,128)(2,1)S(1)} %bitcast.71, bf16[2048,4096]{1,0:T(8,128)(2,1)} %all-gather.2.cloned.1.call-done), kind=kOutput, calls=%fused_computation.34 | convolution fusion | flops 4296015872 | bytes 19922944 | tf_op jit(solution)/shard_map/dot_general | solution.py:104
  468.5 27.2 %all_to_all.5 = bf16[2,256,2048]{2,1,0:T(8,128)(2,1)S(1)} all-to-all(bf16[2,256,2048]{2,1,0:T(8,128)(2,1)S(1)} %bitcast.70), channel_id=1, replica_groups=mesh['groups'=4,'ctx'=32,'tp'=2] {'tp'}, dimensions={0} | all-to-all | bytes 4194304 | tf_op jit(solution)/shard_map/all_to_all | solution.py:25
  (675 shorter events, 229.0 us)
Async XLA Ops:
  6.5 453.4 %all-gather.2.cloned.1.call-start = ((), (), s32[]{:S(2)}) async-start(), calls=%async_computation.1 | async-start | bytes 17301504 | tf_op jit(solution)/shard_map/all_gather | solution.py:106
  19.4 28.9 %collective-permute-start = (bf16[256,2,128]{2,0,1:T(8,128)(2,1)}, bf16[256,2,128]{2,0,1:T(8,128)(2,1)S(1)}, u32[]{:S(2)}, u32[]{:S(2)}) collective-permute-start(bf16[256,2,128]{2,0,1:T(8,128)(2,1)} %get-tuple-element.208), channel_id=1, source_target_pairs={{0,2},{2,4},{4,6},{6,8},{8,10},{10,12},{12,14},{14,16},{16,18},{18... | collective-permute-start | bytes 393224 | tf_op jit(solution)/shard_map/while/body/eval_jaxpr/ppermute | solution.py:15
  22.2 24.4 %collective-permute-start.2 = (s32[256]{0:T(256)S(1)}, s32[256]{0:T(256)S(1)}, u32[]{:S(2)}, u32[]{:S(2)}) collective-permute-start(s32[256]{0:T(256)S(1)} %get-tuple-element.210), channel_id=1, source_target_pairs={{0,2},{2,4},{4,6},{6,8},{8,10},{10,12},{12,14},{14,16},{16,18},{18... | collective-permute-start | bytes 3080 | tf_op jit(solution)/shard_map/while/body/eval_jaxpr/ppermute | solution.py:15
  24.1 26.1 %collective-permute-start.1 = (bf16[256,2,128]{2,0,1:T(8,128)(2,1)}, bf16[256,2,128]{2,0,1:T(8,128)(2,1)S(1)}, u32[]{:S(2)}, u32[]{:S(2)}) collective-permute-start(bf16[256,2,128]{2,0,1:T(8,128)(2,1)} %get-tuple-element.209), channel_id=1, source_target_pairs={{0,2},{2,4},{4,6},{6,8},{8,10},{10,12},{12,14},{14,16},{16,18},{18... | collective-permute-start | bytes 393224 | tf_op jit(solution)/shard_map/while/body/eval_jaxpr/ppermute | solution.py:15
  74.3 10.0 %collective-permute-start = (bf16[256,2,128]{2,0,1:T(8,128)(2,1)}, bf16[256,2,128]{2,0,1:T(8,128)(2,1)S(1)}, u32[]{:S(2)}, u32[]{:S(2)}) collective-permute-start(bf16[256,2,128]{2,0,1:T(8,128)(2,1)} %get-tuple-element.208), channel_id=1, source_target_pairs={{0,2},{2,4},{4,6},{6,8},{8,10},{10,12},{12,14},{14,16},{16,18},{18... | collective-permute-start | bytes 393224 | tf_op jit(solution)/shard_map/while/body/eval_jaxpr/ppermute | solution.py:15
  74.5 12.2 %collective-permute-start.1 = (bf16[256,2,128]{2,0,1:T(8,128)(2,1)}, bf16[256,2,128]{2,0,1:T(8,128)(2,1)S(1)}, u32[]{:S(2)}, u32[]{:S(2)}) collective-permute-start(bf16[256,2,128]{2,0,1:T(8,128)(2,1)} %get-tuple-element.209), channel_id=1, source_target_pairs={{0,2},{2,4},{4,6},{6,8},{8,10},{10,12},{12,14},{14,16},{16,18},{18... | collective-permute-start | bytes 393224 | tf_op jit(solution)/shard_map/while/body/eval_jaxpr/ppermute | solution.py:15
  88.8 10.5 %collective-permute-start = (bf16[256,2,128]{2,0,1:T(8,128)(2,1)}, bf16[256,2,128]{2,0,1:T(8,128)(2,1)S(1)}, u32[]{:S(2)}, u32[]{:S(2)}) collective-permute-start(bf16[256,2,128]{2,0,1:T(8,128)(2,1)} %get-tuple-element.208), channel_id=1, source_target_pairs={{0,2},{2,4},{4,6},{6,8},{8,10},{10,12},{12,14},{14,16},{16,18},{18... | collective-permute-start | bytes 393224 | tf_op jit(solution)/shard_map/while/body/eval_jaxpr/ppermute | solution.py:15
  89.0 11.9 %collective-permute-start.1 = (bf16[256,2,128]{2,0,1:T(8,128)(2,1)}, bf16[256,2,128]{2,0,1:T(8,128)(2,1)S(1)}, u32[]{:S(2)}, u32[]{:S(2)}) collective-permute-start(bf16[256,2,128]{2,0,1:T(8,128)(2,1)} %get-tuple-element.209), channel_id=1, source_target_pairs={{0,2},{2,4},{4,6},{6,8},{8,10},{10,12},{12,14},{14,16},{16,18},{18... | collective-permute-start | bytes 393224 | tf_op jit(solution)/shard_map/while/body/eval_jaxpr/ppermute | solution.py:15
  103.2 11.4 %collective-permute-start.1 = (bf16[256,2,128]{2,0,1:T(8,128)(2,1)}, bf16[256,2,128]{2,0,1:T(8,128)(2,1)S(1)}, u32[]{:S(2)}, u32[]{:S(2)}) collective-permute-start(bf16[256,2,128]{2,0,1:T(8,128)(2,1)} %get-tuple-element.209), channel_id=1, source_target_pairs={{0,2},{2,4},{4,6},{6,8},{8,10},{10,12},{12,14},{14,16},{16,18},{18... | collective-permute-start | bytes 393224 | tf_op jit(solution)/shard_map/while/body/eval_jaxpr/ppermute | solution.py:15
  116.6 10.9 %collective-permute-start = (bf16[256,2,128]{2,0,1:T(8,128)(2,1)}, bf16[256,2,128]{2,0,1:T(8,128)(2,1)S(1)}, u32[]{:S(2)}, u32[]{:S(2)}) collective-permute-start(bf16[256,2,128]{2,0,1:T(8,128)(2,1)} %get-tuple-element.208), channel_id=1, source_target_pairs={{0,2},{2,4},{4,6},{6,8},{8,10},{10,12},{12,14},{14,16},{16,18},{18... | collective-permute-start | bytes 393224 | tf_op jit(solution)/shard_map/while/body/eval_jaxpr/ppermute | solution.py:15
  116.9 12.5 %collective-permute-start.1 = (bf16[256,2,128]{2,0,1:T(8,128)(2,1)}, bf16[256,2,128]{2,0,1:T(8,128)(2,1)S(1)}, u32[]{:S(2)}, u32[]{:S(2)}) collective-permute-start(bf16[256,2,128]{2,0,1:T(8,128)(2,1)} %get-tuple-element.209), channel_id=1, source_target_pairs={{0,2},{2,4},{4,6},{6,8},{8,10},{10,12},{12,14},{14,16},{16,18},{18... | collective-permute-start | bytes 393224 | tf_op jit(solution)/shard_map/while/body/eval_jaxpr/ppermute | solution.py:15
  131.3 11.5 %collective-permute-start = (bf16[256,2,128]{2,0,1:T(8,128)(2,1)}, bf16[256,2,128]{2,0,1:T(8,128)(2,1)S(1)}, u32[]{:S(2)}, u32[]{:S(2)}) collective-permute-start(bf16[256,2,128]{2,0,1:T(8,128)(2,1)} %get-tuple-element.208), channel_id=1, source_target_pairs={{0,2},{2,4},{4,6},{6,8},{8,10},{10,12},{12,14},{14,16},{16,18},{18... | collective-permute-start | bytes 393224 | tf_op jit(solution)/shard_map/while/body/eval_jaxpr/ppermute | solution.py:15
  131.6 12.9 %collective-permute-start.1 = (bf16[256,2,128]{2,0,1:T(8,128)(2,1)}, bf16[256,2,128]{2,0,1:T(8,128)(2,1)S(1)}, u32[]{:S(2)}, u32[]{:S(2)}) collective-permute-start(bf16[256,2,128]{2,0,1:T(8,128)(2,1)} %get-tuple-element.209), channel_id=1, source_target_pairs={{0,2},{2,4},{4,6},{6,8},{8,10},{10,12},{12,14},{14,16},{16,18},{18... | collective-permute-start | bytes 393224 | tf_op jit(solution)/shard_map/while/body/eval_jaxpr/ppermute | solution.py:15
  146.6 11.7 %collective-permute-start = (bf16[256,2,128]{2,0,1:T(8,128)(2,1)}, bf16[256,2,128]{2,0,1:T(8,128)(2,1)S(1)}, u32[]{:S(2)}, u32[]{:S(2)}) collective-permute-start(bf16[256,2,128]{2,0,1:T(8,128)(2,1)} %get-tuple-element.208), channel_id=1, source_target_pairs={{0,2},{2,4},{4,6},{6,8},{8,10},{10,12},{12,14},{14,16},{16,18},{18... | collective-permute-start | bytes 393224 | tf_op jit(solution)/shard_map/while/body/eval_jaxpr/ppermute | solution.py:15
  146.8 13.1 %collective-permute-start.1 = (bf16[256,2,128]{2,0,1:T(8,128)(2,1)}, bf16[256,2,128]{2,0,1:T(8,128)(2,1)S(1)}, u32[]{:S(2)}, u32[]{:S(2)}) collective-permute-start(bf16[256,2,128]{2,0,1:T(8,128)(2,1)} %get-tuple-element.209), channel_id=1, source_target_pairs={{0,2},{2,4},{4,6},{6,8},{8,10},{10,12},{12,14},{14,16},{16,18},{18... | collective-permute-start | bytes 393224 | tf_op jit(solution)/shard_map/while/body/eval_jaxpr/ppermute | solution.py:15
  162.0 11.5 %collective-permute-start = (bf16[256,2,128]{2,0,1:T(8,128)(2,1)}, bf16[256,2,128]{2,0,1:T(8,128)(2,1)S(1)}, u32[]{:S(2)}, u32[]{:S(2)}) collective-permute-start(bf16[256,2,128]{2,0,1:T(8,128)(2,1)} %get-tuple-element.208), channel_id=1, source_target_pairs={{0,2},{2,4},{4,6},{6,8},{8,10},{10,12},{12,14},{14,16},{16,18},{18... | collective-permute-start | bytes 393224 | tf_op jit(solution)/shard_map/while/body/eval_jaxpr/ppermute | solution.py:15
  162.2 13.8 %collective-permute-start.1 = (bf16[256,2,128]{2,0,1:T(8,128)(2,1)}, bf16[256,2,128]{2,0,1:T(8,128)(2,1)S(1)}, u32[]{:S(2)}, u32[]{:S(2)}) collective-permute-start(bf16[256,2,128]{2,0,1:T(8,128)(2,1)} %get-tuple-element.209), channel_id=1, source_target_pairs={{0,2},{2,4},{4,6},{6,8},{8,10},{10,12},{12,14},{14,16},{16,18},{18... | collective-permute-start | bytes 393224 | tf_op jit(solution)/shard_map/while/body/eval_jaxpr/ppermute | solution.py:15
  178.0 11.7 %collective-permute-start = (bf16[256,2,128]{2,0,1:T(8,128)(2,1)}, bf16[256,2,128]{2,0,1:T(8,128)(2,1)S(1)}, u32[]{:S(2)}, u32[]{:S(2)}) collective-permute-start(bf16[256,2,128]{2,0,1:T(8,128)(2,1)} %get-tuple-element.208), channel_id=1, source_target_pairs={{0,2},{2,4},{4,6},{6,8},{8,10},{10,12},{12,14},{14,16},{16,18},{18... | collective-permute-start | bytes 393224 | tf_op jit(solution)/shard_map/while/body/eval_jaxpr/ppermute | solution.py:15
  178.3 14.3 %collective-permute-start.1 = (bf16[256,2,128]{2,0,1:T(8,128)(2,1)}, bf16[256,2,128]{2,0,1:T(8,128)(2,1)S(1)}, u32[]{:S(2)}, u32[]{:S(2)}) collective-permute-start(bf16[256,2,128]{2,0,1:T(8,128)(2,1)} %get-tuple-element.209), channel_id=1, source_target_pairs={{0,2},{2,4},{4,6},{6,8},{8,10},{10,12},{12,14},{14,16},{16,18},{18... | collective-permute-start | bytes 393224 | tf_op jit(solution)/shard_map/while/body/eval_jaxpr/ppermute | solution.py:15
  194.6 10.3 %collective-permute-start = (bf16[256,2,128]{2,0,1:T(8,128)(2,1)}, bf16[256,2,128]{2,0,1:T(8,128)(2,1)S(1)}, u32[]{:S(2)}, u32[]{:S(2)}) collective-permute-start(bf16[256,2,128]{2,0,1:T(8,128)(2,1)} %get-tuple-element.208), channel_id=1, source_target_pairs={{0,2},{2,4},{4,6},{6,8},{8,10},{10,12},{12,14},{14,16},{16,18},{18... | collective-permute-start | bytes 393224 | tf_op jit(solution)/shard_map/while/body/eval_jaxpr/ppermute | solution.py:15
  194.8 11.7 %collective-permute-start.1 = (bf16[256,2,128]{2,0,1:T(8,128)(2,1)}, bf16[256,2,128]{2,0,1:T(8,128)(2,1)S(1)}, u32[]{:S(2)}, u32[]{:S(2)}) collective-permute-start(bf16[256,2,128]{2,0,1:T(8,128)(2,1)} %get-tuple-element.209), channel_id=1, source_target_pairs={{0,2},{2,4},{4,6},{6,8},{8,10},{10,12},{12,14},{14,16},{16,18},{18... | collective-permute-start | bytes 393224 | tf_op jit(solution)/shard_map/while/body/eval_jaxpr/ppermute | solution.py:15
  209.2 10.7 %collective-permute-start.1 = (bf16[256,2,128]{2,0,1:T(8,128)(2,1)}, bf16[256,2,128]{2,0,1:T(8,128)(2,1)S(1)}, u32[]{:S(2)}, u32[]{:S(2)}) collective-permute-start(bf16[256,2,128]{2,0,1:T(8,128)(2,1)} %get-tuple-element.209), channel_id=1, source_target_pairs={{0,2},{2,4},{4,6},{6,8},{8,10},{10,12},{12,14},{14,16},{16,18},{18... | collective-permute-start | bytes 393224 | tf_op jit(solution)/shard_map/while/body/eval_jaxpr/ppermute | solution.py:15
  221.8 10.9 %collective-permute-start = (bf16[256,2,128]{2,0,1:T(8,128)(2,1)}, bf16[256,2,128]{2,0,1:T(8,128)(2,1)S(1)}, u32[]{:S(2)}, u32[]{:S(2)}) collective-permute-start(bf16[256,2,128]{2,0,1:T(8,128)(2,1)} %get-tuple-element.208), channel_id=1, source_target_pairs={{0,2},{2,4},{4,6},{6,8},{8,10},{10,12},{12,14},{14,16},{16,18},{18... | collective-permute-start | bytes 393224 | tf_op jit(solution)/shard_map/while/body/eval_jaxpr/ppermute | solution.py:15
  224.3 11.7 %collective-permute-start.1 = (bf16[256,2,128]{2,0,1:T(8,128)(2,1)}, bf16[256,2,128]{2,0,1:T(8,128)(2,1)S(1)}, u32[]{:S(2)}, u32[]{:S(2)}) collective-permute-start(bf16[256,2,128]{2,0,1:T(8,128)(2,1)} %get-tuple-element.209), channel_id=1, source_target_pairs={{0,2},{2,4},{4,6},{6,8},{8,10},{10,12},{12,14},{14,16},{16,18},{18... | collective-permute-start | bytes 393224 | tf_op jit(solution)/shard_map/while/body/eval_jaxpr/ppermute | solution.py:15
  238.8 11.5 %collective-permute-start.1 = (bf16[256,2,128]{2,0,1:T(8,128)(2,1)}, bf16[256,2,128]{2,0,1:T(8,128)(2,1)S(1)}, u32[]{:S(2)}, u32[]{:S(2)}) collective-permute-start(bf16[256,2,128]{2,0,1:T(8,128)(2,1)} %get-tuple-element.209), channel_id=1, source_target_pairs={{0,2},{2,4},{4,6},{6,8},{8,10},{10,12},{12,14},{14,16},{16,18},{18... | collective-permute-start | bytes 393224 | tf_op jit(solution)/shard_map/while/body/eval_jaxpr/ppermute | solution.py:15
  252.6 11.0 %collective-permute-start.1 = (bf16[256,2,128]{2,0,1:T(8,128)(2,1)}, bf16[256,2,128]{2,0,1:T(8,128)(2,1)S(1)}, u32[]{:S(2)}, u32[]{:S(2)}) collective-permute-start(bf16[256,2,128]{2,0,1:T(8,128)(2,1)} %get-tuple-element.209), channel_id=1, source_target_pairs={{0,2},{2,4},{4,6},{6,8},{8,10},{10,12},{12,14},{14,16},{16,18},{18... | collective-permute-start | bytes 393224 | tf_op jit(solution)/shard_map/while/body/eval_jaxpr/ppermute | solution.py:15
  266.4 11.5 %collective-permute-start.1 = (bf16[256,2,128]{2,0,1:T(8,128)(2,1)}, bf16[256,2,128]{2,0,1:T(8,128)(2,1)S(1)}, u32[]{:S(2)}, u32[]{:S(2)}) collective-permute-start(bf16[256,2,128]{2,0,1:T(8,128)(2,1)} %get-tuple-element.209), channel_id=1, source_target_pairs={{0,2},{2,4},{4,6},{6,8},{8,10},{10,12},{12,14},{14,16},{16,18},{18... | collective-permute-start | bytes 393224 | tf_op jit(solution)/shard_map/while/body/eval_jaxpr/ppermute | solution.py:15
  319.4 10.0 %collective-permute-start = (bf16[256,2,128]{2,0,1:T(8,128)(2,1)}, bf16[256,2,128]{2,0,1:T(8,128)(2,1)S(1)}, u32[]{:S(2)}, u32[]{:S(2)}) collective-permute-start(bf16[256,2,128]{2,0,1:T(8,128)(2,1)} %get-tuple-element.208), channel_id=1, source_target_pairs={{0,2},{2,4},{4,6},{6,8},{8,10},{10,12},{12,14},{14,16},{16,18},{18... | collective-permute-start | bytes 393224 | tf_op jit(solution)/shard_map/while/body/eval_jaxpr/ppermute | solution.py:15
  333.9 10.4 %collective-permute-start = (bf16[256,2,128]{2,0,1:T(8,128)(2,1)}, bf16[256,2,128]{2,0,1:T(8,128)(2,1)S(1)}, u32[]{:S(2)}, u32[]{:S(2)}) collective-permute-start(bf16[256,2,128]{2,0,1:T(8,128)(2,1)} %get-tuple-element.208), channel_id=1, source_target_pairs={{0,2},{2,4},{4,6},{6,8},{8,10},{10,12},{12,14},{14,16},{16,18},{18... | collective-permute-start | bytes 393224 | tf_op jit(solution)/shard_map/while/body/eval_jaxpr/ppermute | solution.py:15
  336.2 10.2 %collective-permute-start.1 = (bf16[256,2,128]{2,0,1:T(8,128)(2,1)}, bf16[256,2,128]{2,0,1:T(8,128)(2,1)S(1)}, u32[]{:S(2)}, u32[]{:S(2)}) collective-permute-start(bf16[256,2,128]{2,0,1:T(8,128)(2,1)} %get-tuple-element.209), channel_id=1, source_target_pairs={{0,2},{2,4},{4,6},{6,8},{8,10},{10,12},{12,14},{14,16},{16,18},{18... | collective-permute-start | bytes 393224 | tf_op jit(solution)/shard_map/while/body/eval_jaxpr/ppermute | solution.py:15
  431.7 10.0 %collective-permute-start.1 = (bf16[256,2,128]{2,0,1:T(8,128)(2,1)}, bf16[256,2,128]{2,0,1:T(8,128)(2,1)S(1)}, u32[]{:S(2)}, u32[]{:S(2)}) collective-permute-start(bf16[256,2,128]{2,0,1:T(8,128)(2,1)} %get-tuple-element.209), channel_id=1, source_target_pairs={{0,2},{2,4},{4,6},{6,8},{8,10},{10,12},{12,14},{14,16},{16,18},{18... | collective-permute-start | bytes 393224 | tf_op jit(solution)/shard_map/while/body/eval_jaxpr/ppermute | solution.py:15
  444.0 10.2 %collective-permute-start.1 = (bf16[256,2,128]{2,0,1:T(8,128)(2,1)}, bf16[256,2,128]{2,0,1:T(8,128)(2,1)S(1)}, u32[]{:S(2)}, u32[]{:S(2)}) collective-permute-start(bf16[256,2,128]{2,0,1:T(8,128)(2,1)} %get-tuple-element.209), channel_id=1, source_target_pairs={{0,2},{2,4},{4,6},{6,8},{8,10},{10,12},{12,14},{14,16},{16,18},{18... | collective-permute-start | bytes 393224 | tf_op jit(solution)/shard_map/while/body/eval_jaxpr/ppermute | solution.py:15
  (64 other events, 494.9 us)
Sparse Core Ops, SparseCore 0:
  9.1 341.5 all-gather.1
where the time goes:
time: 510 us; the launch traced here: 504 us
  waiting for transfers between devices  200 us (39%)
  matrix products  73.7 us (14%)
  starting transfers between devices  69 us (14%)
  local copies, waits for them, and re-layouts  65 us (13%)
  loops' own time  40.8 us (8%)
  blocking collectives  27.2 us (5%)
  other arithmetic  15.6 us (3%)
  between operations  13.5 us (3%)
    ppermute x93, waiting for transfers between devices, from_behind(): lax.ppermute(value, axis, [(i, (i + by) % devices) for i in range(devices)])  199 us
    ppermute x93, starting transfers between devices, from_behind(): lax.ppermute(value, axis, [(i, (i + by) % devices) for i in range(devices)])  69 us
    dot_general x63, matrix products, attend_block(): jnp.einsum('kgqs,skd->kgqd', exp_scores.astype(jnp.bfloat16), value_part,...  44.4 us
    another operation x1, loops' own time, local(): lax.fori_loop(0, lax.axis_size('ctx') - 1, forward_turn, (own_block, part...  40.8 us
    while x155, local copies, waits for them, and re-layouts  40.4 us
    all_to_all x1, blocking collectives, sent_and_summed(): lax.all_to_all(parts, axis, split_axis=0, concat_axis=0, tiled=True)  27.2 us
    dot_general x63, matrix products, attend_block(): jnp.einsum('qkgd,skd->kgqs', query_part, key_part, preferred_element_type...  20.9 us
    slice x31, local copies, waits for them, and re-layouts, remote_step(): key_places[0] < own_first  15.7 us
  transfers between devices with their start and end apart: 94, of which 45 were waited for; matrix products, arithmetic and copies ran while one was open for 28% of the time, Pallas kernels for 0%

commit v1 on v0

v1 whole, which is shorter than its diff:
```python
import functools

import jax
import jax.numpy as jnp
from jax import lax
from jax.experimental import pallas as pl
from jax.experimental.pallas import tpu as pltpu
from jax.sharding import PartitionSpec as P

MESH = pl.DeviceIdType.MESH
LOG2E = 1.4426950408889634
LOW = -1e30
HIGH = 1e30
TAG_ROWS = 16
LANES = 256


def flip(index, stride):
    return index + stride * (1 - 2 * lax.rem(index // stride, 2))


def kernel(
    n, row_stride, kv_heads, half, q_hbm, k_hbm, v_hbm, w_hbm, out_ref,
    q_ref, kbuf, vbuf, wbuf, acc_ref, max_ref, sum_ref, att_ref, give_ref, take_ref,
    in_sem, k_send, v_send, w_send, x_send, y_send, xd_send, yd_send,
    k_recv, v_recv, w_recv, w_last_recv, x_recv, y_recv, xd_recv, yd_recv, give_send, take_recv,
):
    me, group, core = (lax.axis_index(a) for a in ("ctx", "groups", "tp"))
    head_size = q_ref.shape[2]
    width = q_ref.shape[3]
    chunks = width // LANES
    keys = 2 * half
    scale = LOG2E * head_size ** (-0.5)
    rows = wbuf.shape[1]
    quarter, eighth = rows // 4, rows // 8
    steps = n // 2

    right, left = lax.rem(me + 1, n), lax.rem(me + n - 1, n)
    x_group, y_group = flip(group, 1), flip(group, row_stride)
    px, py = lax.rem(group, 2), lax.rem(group // row_stride, 2)
    mine = pl.multiple_of((2 * py + px) * quarter, quarter)
    of_x = pl.multiple_of((2 * py + 1 - px) * quarter, quarter)
    of_y = pl.multiple_of((2 * (1 - py) + px) * quarter, quarter)
    of_xy = pl.multiple_of((2 * (1 - py) + 1 - px) * quarter, quarter)
    to_right, to_left = {"ctx": right}, {"ctx": left}
    to_x, to_y, to_twin = {"groups": x_group}, {"groups": y_group}, {"tp": 1 - core}

    def remote(ref, send, recv, device):
        return pltpu.make_async_remote_copy(
            src_ref=ref, dst_ref=ref, send_sem=send, recv_sem=recv, device_id=device, device_id_type=MESH
        )

    def way(d):
        return to_right if d == 0 else to_left

    def k_copy(d, slot):
        return remote(kbuf.at[slot], k_send.at[d, slot], k_recv.at[slot], way(d))

    def v_copy(d, slot):
        return remote(vbuf.at[slot], v_send.at[d, slot], v_recv.at[slot], way(d))

    def w_copy(d, slot):
        return remote(wbuf.at[slot, pl.ds(mine, quarter)], w_send.at[d, slot], w_recv.at[slot], way(d))

    def w_last_copy(d, slot):
        ref = wbuf.at[slot, pl.ds(mine + d * eighth, eighth)]
        return remote(ref, w_send.at[d, slot], w_recv.at[slot] if d == 0 else w_last_recv.at[0], way(d))

    def x_copy(slot, start):
        return remote(wbuf.at[slot, pl.ds(start, quarter)], x_send.at[slot], x_recv.at[slot], to_x)

    def y_copy(slot, start):
        return remote(wbuf.at[slot, pl.ds(start, quarter)], y_send.at[slot], y_recv.at[slot], to_y)

    def xd_copy(slot, start):
        return remote(wbuf.at[slot, pl.ds(start, eighth)], xd_send.at[slot], xd_recv.at[slot], to_x)

    def yd_copy(slot, start):
        return remote(wbuf.at[slot, pl.ds(start + eighth, eighth)], yd_send.at[slot], yd_recv.at[slot], to_y)

    def side(slot):
        x_copy(slot, mine).start()
        y_copy(slot, mine).start()

    def relay(slot):
        x_copy(slot, of_x).wait_recv()
        yd_copy(slot, of_x).start()
        y_copy(slot, of_y).wait_recv()
        xd_copy(slot, of_y).start()

    own = (
        pltpu.make_async_copy(k_hbm, kbuf.at[me], in_sem.at[0]),
        pltpu.make_async_copy(v_hbm, vbuf.at[me], in_sem.at[1]),
        pltpu.make_async_copy(w_hbm, wbuf.at[me], in_sem.at[2]),
        pltpu.make_async_copy(q_hbm, q_ref, in_sem.at[3]),
    )
    for copy in own:
        copy.start()

    barrier = pltpu.get_barrier_semaphore()
    for device in (to_right, to_left, to_x, to_y, to_twin):
        pl.semaphore_signal(barrier, inc=1, device_id=device, device_id_type=MESH)
    pl.semaphore_wait(barrier, 5)

    own[0].wait()
    for d in (0, 1):
        k_copy(d, me).start()
    own[1].wait()
    for d in (0, 1):
        v_copy(d, me).start()
    own[2].wait()
    for d in (0, 1):
        w_copy(d, me).start()
    own[3].wait()

    def places(i):
        kv = i // chunks
        return kv, pl.ds(pl.multiple_of(lax.rem(i, chunks) * LANES, LANES), LANES)

    def scores_of(key_part, kv, part, lanes):
        return jnp.dot(key_part, q_ref[kv, part, :, lanes], preferred_element_type=jnp.float32)

    def powers(scores, shift):
        return jnp.exp2((scores - shift) * scale)

    def column_max(scores):
        return jnp.max(scores, axis=0, keepdims=True)

    def column_sum(values):
        return jnp.sum(values, axis=0, keepdims=True)

    def first(i, _):
        kv, lanes = places(i)
        key_rows = pl.multiple_of(kv * keys, keys)
        key_block = kbuf[me, pl.ds(key_rows, keys), :]
        values = vbuf[me, kv]
        shape = (half, LANES)
        tri = lax.broadcasted_iota(jnp.int32, shape, 0) <= lax.rem(lax.broadcasted_iota(jnp.int32, shape, 1), half)
        for part in (0, 1):
            scores = scores_of(key_block[: half * (part + 1)], kv, part, lanes)
            pieces = [scores[half * j : half * (j + 1)] for j in range(part + 1)]
            pieces[part] = jnp.where(tri, pieces[part], LOW)
            largest = functools.reduce(jnp.maximum, [column_max(p) for p in pieces])
            exps = jnp.concatenate([powers(p, largest) for p in pieces], axis=0)
            max_ref[kv, part, :, lanes] = largest
            sum_ref[kv, part, :, lanes] = column_sum(exps)
            acc_ref[kv, part, :, lanes] = jnp.dot(
                values[:, : half * (part + 1)], exps.astype(jnp.bfloat16), preferred_element_type=jnp.float32
            )
        return 0

    lax.fori_loop(0, kv_heads * chunks, first, 0)

    def tag(slot):
        row = kbuf[slot, kv_heads * keys :, :].astype(jnp.float32)[:1]
        return jnp.concatenate([row] * (LANES // row.shape[1]), axis=1)

    def attend(slot):
        theirs, ours = tag(slot), tag(me)
        before, after = theirs < ours, theirs > ours

        def one(i, _):
            kv, lanes = places(i)
            key_rows = pl.multiple_of(kv * keys, keys)
            key_block = kbuf[slot, pl.ds(key_rows, keys), :]
            values = vbuf[slot, kv]

            def renew(part, largest, shifts, pieces, value_part):
                old = max_ref[kv, part, :, lanes]
                factor = jnp.exp2((old - largest) * scale)
                exps = jnp.concatenate([powers(p, s) for p, s in zip(pieces, shifts)], axis=0)
                max_ref[kv, part, :, lanes] = largest
                sum_ref[kv, part, :, lanes] = sum_ref[kv, part, :, lanes] * factor + column_sum(exps)
                acc_ref[kv, part, :, lanes] = acc_ref[kv, part, :, lanes] * factor + jnp.dot(
                    value_part, exps.astype(jnp.bfloat16), preferred_element_type=jnp.float32
                )

            low = scores_of(key_block[:half], kv, 0, lanes)
            largest = jnp.maximum(max_ref[kv, 0, :, lanes], jnp.where(before, column_max(low), LOW))
            renew(0, largest, [jnp.where(before, largest, HIGH)], [low], values[:, :half])

            high = scores_of(key_block, kv, 1, lanes)
            pieces = [high[:half], high[half:]]
            largest = jnp.maximum(column_max(pieces[0]), jnp.where(after, column_max(pieces[1]), LOW))
            largest = jnp.maximum(max_ref[kv, 1, :, lanes], largest)
            renew(1, largest, [largest, jnp.where(after, largest, HIGH)], pieces, values)
            return 0

        lax.fori_loop(0, kv_heads * chunks, one, 0)

    def behind(s):
        return lax.rem(me + n - s, n)

    def ahead(s):
        return lax.rem(me + s, n)

    def step(s, _):
        a, b = behind(s), ahead(s)
        k_copy(0, a).wait_recv()
        k_copy(0, a).start()
        k_copy(1, b).wait_recv()

        @pl.when(s < steps - 1)
        def _():
            k_copy(1, b).start()

        v_copy(0, a).wait_recv()

        @pl.when(s < steps - 1)
        def _():
            v_copy(0, a).start()

        v_copy(1, b).wait_recv()
        v_copy(1, b).start()
        attend(a)

        w_copy(0, a).wait_recv()
        w_copy(1, b).wait_recv()

        @pl.when(s < steps - 1)
        def _():
            w_copy(0, a).start()
            w_copy(1, b).start()

        @pl.when(s == steps - 1)
        def _():
            w_last_copy(0, a).start()
            w_last_copy(1, b).start()

        side(a)
        side(b)

        @pl.when(s > 1)
        def _():
            relay(behind(s - 1))
            relay(ahead(s - 1))

        attend(b)
        return 0

    lax.fori_loop(1, steps, step, 0)

    far = ahead(steps)
    k_copy(0, far).wait_recv()
    v_copy(1, far).wait_recv()
    relay(behind(steps - 1))
    relay(ahead(steps - 1))
    attend(far)
    w_last_copy(0, far).wait_recv()
    w_last_copy(1, far).wait_recv()
    side(far)

    heads = width // half

    def finish(i, _):
        kv, part = i // 2, lax.rem(i, 2)
        for h in range(heads):
            lanes = slice(h * half, (h + 1) * half)
            tile = acc_ref[kv, part, :, lanes] / sum_ref[kv, part, :, lanes]
            columns = pl.ds(pl.multiple_of((kv * heads + h) * head_size, head_size), head_size)
            att_ref[pl.ds(pl.multiple_of(part * half, half), half), columns] = tile.T.astype(jnp.bfloat16)
        return 0

    lax.fori_loop(0, kv_heads * 2, finish, 0)

    relay(far)

    def arrived(s, _):
        slot = ahead(s)
        xd_copy(slot, of_xy).wait_recv()
        yd_copy(slot, of_xy).wait_recv()
        return 0

    lax.fori_loop(1, n, arrived, 0)

    pairs = n // 4

    def product(pair):
        weight = jnp.concatenate([wbuf[2 * pair], wbuf[2 * pair + 1]], axis=1)
        return jnp.dot(att_ref[...], weight, preferred_element_type=jnp.float32)

    def give_copy(i):
        return pltpu.make_async_remote_copy(
            src_ref=give_ref.at[i], dst_ref=take_ref.at[i], send_sem=give_send.at[i], recv_sem=take_recv.at[i],
            device_id=to_twin, device_id_type=MESH,
        )

    def give(i, _):
        give_ref[i] = product((1 - core) * pairs + i).astype(jnp.bfloat16)

        @pl.when(i > 0)
        def _():
            give_copy(i - 1).start()

        return 0

    lax.fori_loop(0, pairs, give, 0)
    give_copy(pairs - 1).start()

    def keep(i, _):
        total = product(core * pairs + i)
        give_copy(i).wait_recv()
        columns = pl.ds(pl.multiple_of(i * give_ref.shape[2], give_ref.shape[2]), give_ref.shape[2])
        out_ref[:, columns] = (total + take_ref[i].astype(jnp.float32)).astype(jnp.bfloat16)
        return 0

    lax.fori_loop(0, pairs, keep, 0)

    def sent(s, _):
        a, b = behind(s), ahead(s)
        k_copy(0, a).wait_send()
        v_copy(1, b).wait_send()

        @pl.when(s < steps - 1)
        def _():
            k_copy(1, b).wait_send()
            v_copy(0, a).wait_send()
            w_copy(0, a).wait_send()
            w_copy(1, b).wait_send()

        @pl.when(s == steps - 1)
        def _():
            w_last_copy(0, a).wait_send()
            w_last_copy(1, b).wait_send()

        return 0

    lax.fori_loop(1, steps, sent, 0)
    for d in (0, 1):
        for copy in (k_copy, v_copy, w_copy):
            copy(d, me).wait_send()

    def passed(s, _):
        slot = ahead(s)
        x_copy(slot, mine).wait_send()
        y_copy(slot, mine).wait_send()
        yd_copy(slot, of_x).wait_send()
        xd_copy(slot, of_y).wait_send()
        return 0

    lax.fori_loop(1, n, passed, 0)

    def given(i, _):
        give_copy(i).wait_send()
        return 0

    lax.fori_loop(0, pairs, given, 0)


def local(n, row_stride, query_states, key_states, value_rows, positions, out_weight):
    tokens, query_heads, head_size = query_states.shape
    kv_heads = key_states.shape[1]
    heads = query_heads // kv_heads
    half = tokens // 2
    rows, slab = out_weight.shape
    pairs = n // 4
    width = heads * half
    grouped = query_states.reshape(2, half, kv_heads, heads, head_size).transpose(2, 0, 4, 3, 1)
    grouped = grouped.reshape(kv_heads, 2, head_size, width)
    place = (positions[0] // half).astype(jnp.bfloat16)
    tagged = jnp.concatenate(
        [
            key_states.transpose(1, 0, 2).reshape(kv_heads * tokens, head_size),
            jnp.broadcast_to(place, (TAG_ROWS, head_size)),
        ],
        axis=0,
    )
    turned = value_rows.transpose(1, 2, 0)
    dma, bf16, f32 = pltpu.SemaphoreType.DMA, jnp.bfloat16, jnp.float32
    anywhere = pl.BlockSpec(memory_space=pl.ANY)
    return pl.pallas_call(
        functools.partial(kernel, n, row_stride, kv_heads, half),
        out_shape=jax.ShapeDtypeStruct((tokens, n // 2 * slab), bf16),
        in_specs=[anywhere] * 4,
        out_specs=pl.BlockSpec(memory_space=pltpu.VMEM),
        scratch_shapes=[
            pltpu.VMEM(grouped.shape, bf16),
            pltpu.VMEM((n,) + tagged.shape, bf16),
            pltpu.VMEM((n,) + turned.shape, bf16),
            pltpu.VMEM((n, rows, slab), bf16),
            pltpu.VMEM((kv_heads, 2, head_size, width), f32),
            pltpu.VMEM((kv_heads, 2, 1, width), f32),
            pltpu.VMEM((kv_heads, 2, 1, width), f32),
            pltpu.VMEM((tokens, query_heads * head_size), bf16),
            pltpu.VMEM((pairs, tokens, 2 * slab), bf16),
            pltpu.VMEM((pairs, tokens, 2 * slab), bf16),
            dma((4,)),
            dma((2, n)),
            dma((2, n)),
            dma((2, n)),
            dma((n,)),
            dma((n,)),
            dma((n,)),
            dma((n,)),
            dma((n,)),
            dma((n,)),
            dma((n,)),
            dma((1,)),
            dma((n,)),
            dma((n,)),
            dma((n,)),
            dma((n,)),
            dma((pairs,)),
            dma((pairs,)),
        ],
        compiler_params=pltpu.CompilerParams(
            collective_id=0, has_side_effects=True, vmem_limit_bytes=62 * 1024 * 1024
        ),
    )(grouped, tagged, turned, out_weight)


def solution(mesh):
    n, groups = mesh.shape["ctx"], mesh.shape["groups"]
    row_stride = 1 << ((groups.bit_length() - 1) // 2)
    assert n % 4 == 0 and row_stride % 2 == 0 and groups % (2 * row_stride) == 0
    in_specs = (
        P(("groups", "ctx"), "tp", None),
        P(("groups", "ctx"), "tp", None),
        P(("groups", "ctx"), "tp", None),
        P(("groups", "ctx")),
        P("tp", "ctx"),
    )
    out_specs = P(("groups", "ctx"), "tp")
    return jax.shard_map(
        functools.partial(local, n, row_stride),
        mesh=mesh, in_specs=in_specs, out_specs=out_specs, check_vma=False,
    )
```

time: 510 us -> 202 us (0.40); the launches traced: 504 us -> 201 us
  waiting for transfers between devices: 200 us -> 0 us
  Pallas kernels: 0 us -> 189 us
  matrix products: 73.7 us -> 0 us
  starting transfers between devices: 69 us -> 0 us
  local copies, waits for them, and re-layouts: 65 us -> 9.36 us
  loops' own time: 40.8 us -> 0 us
  blocking collectives: 27.2 us -> 0 us
  other arithmetic: 15.6 us -> 0 us
  between operations: 13.5 us -> 2.64 us
    ppermute x93 -> x0, waiting for transfers between devices: 199 us -> none  [from_behind(): lax.ppermute(value, axis, [(i, (i + by) % devices) for i in range(devices)])]
    pallas_call x0 -> x1, Pallas kernels: none -> 189 us  [local(): pl.pallas_call(functools.partial(kernel, n, row_stride, kv_heads, half),...]
    dot_general x127 -> x0, matrix products: 73.7 us -> none  [the longest x63 44.4 us: attend_block(): jnp.einsum('kgqs,skd->kgqd', exp_scores.astype(jnp.bfloat16), value_part,...]
    ppermute x93 -> x0, starting transfers between devices: 69 us -> none  [from_behind(): lax.ppermute(value, axis, [(i, (i + by) % devices) for i in range(devices)])]
    while x158 -> x0, local copies, waits for them, and re-layouts: 44.5 us -> none
    another operation x1 -> x0, loops' own time: 40.8 us -> none  [local(): lax.fori_loop(0, lax.axis_size('ctx') - 1, forward_turn, (own_block, part...]
    all_to_all x1 -> x0, blocking collectives: 27.2 us -> none  [sent_and_summed(): lax.all_to_all(parts, axis, split_axis=0, concat_axis=0, tiled=True)]
    slice x32 -> x1, local copies, waits for them, and re-layouts: 16.2 us -> 1.19 us  [local(): place = (positions[0] // half).astype(jnp.bfloat16)]
  transfers between devices with their start and end apart: 94 -> 0, of which waited for: 45 -> 0; matrix products, arithmetic and copies ran while one was open for 28% -> 0% of each run, Pallas kernels for 0% -> 0%
where the time goes in v1:
time: 202 us; the launch traced here: 201 us
  Pallas kernels  189 us (94%)
  local copies, waits for them, and re-layouts  9.36 us (5%)
  between operations  2.64 us (1%)
    pallas_call x1, Pallas kernels, local(): pl.pallas_call(functools.partial(kernel, n, row_stride, kv_heads, half),...  189 us

profile of v1, /device:TPU:37, one launch (start us, length us, event | category | flops | bytes accessed | tf_op | source)
XLA Modules:
  0.0 201.5 jit_solution(10875242520391005325)
XLA Ops:
  0.0 1.2 slice.3
  3.8 0.9 copy.7
  4.7 0.0 copy-start
  4.7 0.7 concatenate.3.k_hbm
  5.4 0.3 copy-done
  5.7 0.8 copy.8
  6.5 1.9 copy.6
  8.4 1.3 reshape.10.q_hbm
  9.7 189.5 %shard_map.55 = bf16[256,2048]{1,0:T(8,128)(2,1)} custom-call(bf16[2,2,128,1024]{3,2,1,0:T(8,128)(2,1)} %reshape.10.q_hbm, bf16[528,128]{1,0:T(8,128)(2,1)} %concatenate.3.k_hbm, bf16[2,128,256]{2,1,0:T(8,128)(2,1)} %bitcast.10, bf16[2048,128]{1,0:T(8,128)(2,1)} %w_hbm.1), custom_call_target="tpu_custom_call" | custom-call | tf_op jit(solution)/shard_map/pallas_call | solution.py:371
  199.2 2.3 %copy.10 = bf16[256,2048]{1,0:T(8,128)(2,1)} copy(bf16[256,2048]{1,0:T(8,128)(2,1)} %shard_map.55) | data formatting | bytes 2097152
Async XLA Ops:
  4.7 1.0 copy-start

commit v2 on v1

--- a/solution.py
+++ b/solution.py
@@ -12,7 +12,7 @@
 LOW = -1e30
 HIGH = 1e30
 TAG_ROWS = 16
-LANES = 256
+LANES = 1024
 
 
 def flip(index, stride):
@@ -20,8 +20,8 @@
 
 
 def kernel(
-    n, row_stride, kv_heads, half, q_hbm, k_hbm, v_hbm, w_hbm, out_ref,
-    q_ref, kbuf, vbuf, wbuf, acc_ref, max_ref, sum_ref, att_ref, give_ref, take_ref,
+    n, row_stride, kv_heads, half, q_hbm, k_hbm, v_hbm, p_hbm, w_hbm, out_ref,
+    q_raw, k_raw, v_raw, p_raw, q_ref, kbuf, vbuf, wbuf, acc_ref, max_ref, sum_ref, att_ref, give_ref, take_ref,
     in_sem, k_send, v_send, w_send, x_send, y_send, xd_send, yd_send,
     k_recv, v_recv, w_recv, w_last_recv, x_recv, y_recv, xd_recv, yd_recv, give_send, take_recv,
 ):
@@ -89,10 +89,11 @@
         xd_copy(slot, of_y).start()
 
     own = (
-        pltpu.make_async_copy(k_hbm, kbuf.at[me], in_sem.at[0]),
-        pltpu.make_async_copy(v_hbm, vbuf.at[me], in_sem.at[1]),
-        pltpu.make_async_copy(w_hbm, wbuf.at[me], in_sem.at[2]),
-        pltpu.make_async_copy(q_hbm, q_ref, in_sem.at[3]),
+        pltpu.make_async_copy(w_hbm, wbuf.at[me], in_sem.at[0]),
+        pltpu.make_async_copy(k_hbm, k_raw, in_sem.at[1]),
+        pltpu.make_async_copy(p_hbm, p_raw, in_sem.at[2]),
+        pltpu.make_async_copy(v_hbm, v_raw, in_sem.at[3]),
+        pltpu.make_async_copy(q_hbm, q_raw, in_sem.at[4]),
     )
     for copy in own:
         copy.start()
@@ -104,14 +105,30 @@
 
     own[0].wait()
     for d in (0, 1):
+        w_copy(d, me).start()
+
+    own[1].wait()
+    own[2].wait()
+    for kv in range(kv_heads):
+        kbuf[me, kv * keys : (kv + 1) * keys, :] = k_raw[:, kv, :]
+    place = p_raw[0:1, 0:1].astype(jnp.float32) / half
+    kbuf[me, kv_heads * keys :, :] = jnp.broadcast_to(place, (TAG_ROWS, head_size)).astype(jnp.bfloat16)
+    own[3].wait()
+    for kv in range(kv_heads):
+        vbuf[me, kv] = v_raw[:, kv, :].T
+    for d in (0, 1):
         k_copy(d, me).start()
-    own[1].wait()
-    for d in (0, 1):
-        v_copy(d, me).start()
-    own[2].wait()
-    for d in (0, 1):
-        w_copy(d, me).start()
-    own[3].wait()
+
+    own[4].wait()
+    heads = width // half
+    for kv in range(kv_heads):
+        for h in range(heads):
+            turned = q_raw[:, kv * heads + h, :].T
+            for part in (0, 1):
+                q_ref[kv, part, :, h * half : (h + 1) * half] = turned[:, part * half : (part + 1) * half]
+        if kv == 0:
+            for d in (0, 1):
+                v_copy(d, me).start()
 
     def places(i):
         kv = i // chunks
@@ -196,6 +213,26 @@
 
     def step(s, _):
         a, b = behind(s), ahead(s)
+        w_copy(0, a).wait_recv()
+        w_copy(1, b).wait_recv()
+
+        @pl.when(s < steps - 1)
+        def _():
+            w_copy(0, a).start()
+            w_copy(1, b).start()
+
+        @pl.when(s == steps - 1)
+        def _():
+            w_last_copy(0, a).start()
+            w_last_copy(1, b).start()
+
+        side(a)
+        side(b)
+
+        @pl.when(s > 1)
+        def _():
+            attend(ahead(s - 1))
+
         k_copy(0, a).wait_recv()
         k_copy(0, a).start()
         k_copy(1, b).wait_recv()
@@ -212,58 +249,39 @@
 
         v_copy(1, b).wait_recv()
         v_copy(1, b).start()
-        attend(a)
-
-        w_copy(0, a).wait_recv()
-        w_copy(1, b).wait_recv()
-
-        @pl.when(s < steps - 1)
-        def _():
-            w_copy(0, a).start()
-            w_copy(1, b).start()
-
-        @pl.when(s == steps - 1)
-        def _():
-            w_last_copy(0, a).start()
-            w_last_copy(1, b).start()
-
-        side(a)
-        side(b)
 
         @pl.when(s > 1)
         def _():
             relay(behind(s - 1))
             relay(ahead(s - 1))
 
-        attend(b)
+        attend(a)
         return 0
 
     lax.fori_loop(1, steps, step, 0)
 
     far = ahead(steps)
-    k_copy(0, far).wait_recv()
-    v_copy(1, far).wait_recv()
-    relay(behind(steps - 1))
-    relay(ahead(steps - 1))
-    attend(far)
     w_last_copy(0, far).wait_recv()
     w_last_copy(1, far).wait_recv()
     side(far)
-
-    heads = width // half
+    attend(ahead(steps - 1))
+    relay(behind(steps - 1))
+    relay(ahead(steps - 1))
+    k_copy(0, far).wait_recv()
+    v_copy(1, far).wait_recv()
+    attend(far)
+    relay(far)
 
     def finish(i, _):
         kv, part = i // 2, lax.rem(i, 2)
         for h in range(heads):
             lanes = slice(h * half, (h + 1) * half)
-            tile = acc_ref[kv, part, :, lanes] / sum_ref[kv, part, :, lanes]
+            tile = acc_ref[kv, part, :, lanes] * (1.0 / sum_ref[kv, part, :, lanes])
             columns = pl.ds(pl.multiple_of((kv * heads + h) * head_size, head_size), head_size)
             att_ref[pl.ds(pl.multiple_of(part * half, half), half), columns] = tile.T.astype(jnp.bfloat16)
         return 0
 
     lax.fori_loop(0, kv_heads * 2, finish, 0)
-
-    relay(far)
 
     def arrived(s, _):
         slot = ahead(s)
@@ -355,28 +373,21 @@
     rows, slab = out_weight.shape
     pairs = n // 4
     width = heads * half
-    grouped = query_states.reshape(2, half, kv_heads, heads, head_size).transpose(2, 0, 4, 3, 1)
-    grouped = grouped.reshape(kv_heads, 2, head_size, width)
-    place = (positions[0] // half).astype(jnp.bfloat16)
-    tagged = jnp.concatenate(
-        [
-            key_states.transpose(1, 0, 2).reshape(kv_heads * tokens, head_size),
-            jnp.broadcast_to(place, (TAG_ROWS, head_size)),
-        ],
-        axis=0,
-    )
-    turned = value_rows.transpose(1, 2, 0)
     dma, bf16, f32 = pltpu.SemaphoreType.DMA, jnp.bfloat16, jnp.float32
     anywhere = pl.BlockSpec(memory_space=pl.ANY)
     return pl.pallas_call(
         functools.partial(kernel, n, row_stride, kv_heads, half),
         out_shape=jax.ShapeDtypeStruct((tokens, n // 2 * slab), bf16),
-        in_specs=[anywhere] * 4,
+        in_specs=[anywhere] * 5,
         out_specs=pl.BlockSpec(memory_space=pltpu.VMEM),
         scratch_shapes=[
-            pltpu.VMEM(grouped.shape, bf16),
-            pltpu.VMEM((n,) + tagged.shape, bf16),
-            pltpu.VMEM((n,) + turned.shape, bf16),
+            pltpu.VMEM(query_states.shape, bf16),
+            pltpu.VMEM(key_states.shape, bf16),
+            pltpu.VMEM(value_rows.shape, bf16),
+            pltpu.VMEM((2, half), positions.dtype),
+            pltpu.VMEM((kv_heads, 2, head_size, width), bf16),
+            pltpu.VMEM((n, kv_heads * tokens + TAG_ROWS, head_size), bf16),
+            pltpu.VMEM((n, kv_heads, head_size, tokens), bf16),
             pltpu.VMEM((n, rows, slab), bf16),
             pltpu.VMEM((kv_heads, 2, head_size, width), f32),
             pltpu.VMEM((kv_heads, 2, 1, width), f32),
@@ -384,7 +395,7 @@
             pltpu.VMEM((tokens, query_heads * head_size), bf16),
             pltpu.VMEM((pairs, tokens, 2 * slab), bf16),
             pltpu.VMEM((pairs, tokens, 2 * slab), bf16),
-            dma((4,)),
+            dma((5,)),
             dma((2, n)),
             dma((2, n)),
             dma((2, n)),
@@ -406,7 +417,7 @@
         compiler_params=pltpu.CompilerParams(
             collective_id=0, has_side_effects=True, vmem_limit_bytes=62 * 1024 * 1024
         ),
-    )(grouped, tagged, turned, out_weight)
+    )(query_states, key_states, value_rows, positions.reshape(2, half), out_weight)
 
 
 def solution(mesh):

time: 202 us -> 183 us (0.906)
  Pallas kernels: 189 us -> 181 us
  local copies, waits for them, and re-layouts: 9.36 us -> 2.3 us
  between operations: 2.64 us -> 0.01 us
    pallas_call x1, Pallas kernels: 189 us -> 181 us  [local(): pl.pallas_call(functools.partial(kernel, n, row_stride, kv_heads, half),...]
    reshape x2 -> x0, local copies, waits for them, and re-layouts: 3.22 us -> none  [the longest x1 1.95 us: local(): query_states.reshape(2, half, kv_heads, heads, head_size)]
where the time goes in v2:
time: 183 us
  Pallas kernels  181 us (99%)
  local copies, waits for them, and re-layouts  2.3 us (1%)
    pallas_call x1, Pallas kernels, local(): pl.pallas_call(functools.partial(kernel, n, row_stride, kv_heads, half),...  181 us

profile of v2, /device:TPU:37, one launch (start us, length us, event | category | flops | bytes accessed | tf_op | source)
XLA Modules:
  0.0 183.2 jit_solution(18230123503401623093)
XLA Ops:
  0.0 180.8 %shard_map.55 = bf16[256,2048]{1,0:T(8,128)(2,1)} custom-call(bf16[256,16,128]{2,1,0:T(8,128)(2,1)} %q_hbm.1, bf16[256,2,128]{2,1,0:T(2,128)(2,1)} %k_hbm.1, bf16[256,2,128]{2,1,0:T(2,128)(2,1)} %v_hbm.1, s32[2,128]{1,0:T(2,128)} %bitcast.1, bf16[2048,128]{1,0:T(8,128)(2,1)} %w_hbm.1), custom_call_target="tpu_custom_call" | custom-call | tf_op jit(solution)/shard_map/pallas_call | solution.py:378
  180.8 2.3 %copy.7 = bf16[256,2048]{1,0:T(8,128)(2,1)} copy(bf16[256,2048]{1,0:T(8,128)(2,1)} %shard_map.55) | data formatting | bytes 2097152

commit v3 on v2

--- a/solution.py
+++ b/solution.py
@@ -13,6 +13,7 @@
 HIGH = 1e30
 TAG_ROWS = 16
 LANES = 1024
+SLABS = 4
 
 
 def flip(index, stride):
@@ -20,10 +21,10 @@
 
 
 def kernel(
-    n, row_stride, kv_heads, half, q_hbm, k_hbm, v_hbm, p_hbm, w_hbm, out_ref,
-    q_raw, k_raw, v_raw, p_raw, q_ref, kbuf, vbuf, wbuf, acc_ref, max_ref, sum_ref, att_ref, give_ref, take_ref,
+    n, row_stride, kv_heads, half, q_hbm, k_hbm, v_hbm, p_hbm, w_hbm, out_hbm,
+    q_raw, k_raw, v_raw, p_raw, q_ref, kbuf, vbuf, wbuf, acc_ref, max_ref, sum_ref, att_ref, give_ref, take_ref, total_ref,
     in_sem, k_send, v_send, w_send, x_send, y_send, xd_send, yd_send,
-    k_recv, v_recv, w_recv, w_last_recv, x_recv, y_recv, xd_recv, yd_recv, give_send, take_recv,
+    k_recv, v_recv, w_recv, w_last_recv, x_recv, y_recv, xd_recv, yd_recv, give_send, take_recv, out_sem,
 ):
     me, group, core = (lax.axis_index(a) for a in ("ctx", "groups", "tp"))
     head_size = q_ref.shape[2]
@@ -172,12 +173,12 @@
         row = kbuf[slot, kv_heads * keys :, :].astype(jnp.float32)[:1]
         return jnp.concatenate([row] * (LANES // row.shape[1]), axis=1)
 
-    def attend(slot):
+    def attend(slot, kv):
         theirs, ours = tag(slot), tag(me)
         before, after = theirs < ours, theirs > ours
 
         def one(i, _):
-            kv, lanes = places(i)
+            lanes = pl.ds(pl.multiple_of(i * LANES, LANES), LANES)
             key_rows = pl.multiple_of(kv * keys, keys)
             key_block = kbuf[slot, pl.ds(key_rows, keys), :]
             values = vbuf[slot, kv]
@@ -203,13 +204,61 @@
             renew(1, largest, [largest, jnp.where(after, largest, HIGH)], pieces, values)
             return 0
 
-        lax.fori_loop(0, kv_heads * chunks, one, 0)
+        lax.fori_loop(0, chunks, one, 0)
+
+    def attend_all(slot):
+        def one(kv, _):
+            attend(slot, kv)
+            return 0
+
+        lax.fori_loop(0, kv_heads, one, 0)
 
     def behind(s):
         return lax.rem(me + n - s, n)
 
     def ahead(s):
         return lax.rem(me + s, n)
+
+    def arrived_at(slot):
+        xd_copy(slot, of_xy).wait_recv()
+        yd_copy(slot, of_xy).wait_recv()
+
+    def arrived(s):
+        arrived_at(behind(s))
+        arrived_at(ahead(s))
+
+    def sent_aside(slot):
+        x_copy(slot, mine).wait_send()
+        y_copy(slot, mine).wait_send()
+        yd_copy(slot, of_x).wait_send()
+        xd_copy(slot, of_y).wait_send()
+
+    def sent(s):
+        a, b = behind(s), ahead(s)
+        k_copy(0, a).wait_send()
+        v_copy(1, b).wait_send()
+
+        @pl.when(s < steps - 1)
+        def _():
+            k_copy(1, b).wait_send()
+            v_copy(0, a).wait_send()
+            w_copy(0, a).wait_send()
+            w_copy(1, b).wait_send()
+
+        @pl.when(s == steps - 1)
+        def _():
+            w_last_copy(0, a).wait_send()
+            w_last_copy(1, b).wait_send()
+
+        sent_aside(a)
+        sent_aside(b)
+
+    def each(low, high, what):
+        def one(s, _):
+            what(s)
+            return 0
+
+        lax.fori_loop(max(low, 1), high, one, 0)
 
     def step(s, _):
         a, b = behind(s), ahead(s)
@@ -231,7 +280,12 @@
 
         @pl.when(s > 1)
         def _():
-            attend(ahead(s - 1))
+            relay(behind(s - 1))
+            relay(ahead(s - 1))
+
+        @pl.when(s > 1)
+        def _():
+            attend(ahead(s - 1), 0)
 
         k_copy(0, a).wait_recv()
         k_copy(0, a).start()
@@ -241,6 +295,10 @@
         def _():
             k_copy(1, b).start()
 
+        @pl.when(s > 1)
+        def _():
+            attend(ahead(s - 1), 1)
+
         v_copy(0, a).wait_recv()
 
         @pl.when(s < steps - 1)
@@ -250,12 +308,15 @@
         v_copy(1, b).wait_recv()
         v_copy(1, b).start()
 
-        @pl.when(s > 1)
-        def _():
-            relay(behind(s - 1))
-            relay(ahead(s - 1))
-
-        attend(a)
+        @pl.when(s > 2)
+        def _():
+            arrived(s - 2)
+
+        @pl.when(s > 3)
+        def _():
+            sent(s - 3)
+
+        attend_all(a)
         return 0
 
     lax.fori_loop(1, steps, step, 0)
@@ -264,13 +325,12 @@
     w_last_copy(0, far).wait_recv()
     w_last_copy(1, far).wait_recv()
     side(far)
-    attend(ahead(steps - 1))
     relay(behind(steps - 1))
     relay(ahead(steps - 1))
+    attend_all(ahead(steps - 1))
     k_copy(0, far).wait_recv()
     v_copy(1, far).wait_recv()
-    attend(far)
-    relay(far)
+    attend_all(far)
 
     def finish(i, _):
         kv, part = i // 2, lax.rem(i, 2)
@@ -283,86 +343,78 @@
 
     lax.fori_loop(0, kv_heads * 2, finish, 0)
 
-    def arrived(s, _):
-        slot = ahead(s)
-        xd_copy(slot, of_xy).wait_recv()
-        yd_copy(slot, of_xy).wait_recv()
+    relay(far)
+    each(steps - 2, steps, arrived)
+
+    parts = give_ref.shape[0]
+    slabs = n // (2 * parts)
+    span = give_ref.shape[2]
+    far_part = lax.rem(far // slabs, parts)
+    far_given = lax.rem(far // (slabs * parts) + core, 2)
+
+    def turn(i):
+        late = jnp.where(i < parts - 1, i, jnp.where(i < 2 * parts - 1, i + 1, parts - 1))
+        turn = jnp.where(far_given == 1, late, i)
+        return turn < parts, lax.rem(far_part + 1 + lax.rem(turn, parts), parts)
+
+    def give_copy(part):
+        return pltpu.make_async_remote_copy(
+            src_ref=give_ref.at[part], dst_ref=take_ref.at[part], send_sem=give_send.at[part],
+            recv_sem=take_recv.at[part], device_id=to_twin, device_id_type=MESH,
+        )
+
+    def out_copy(part):
+        columns = pl.ds(pl.multiple_of(part * span, span), span)
+        return pltpu.make_async_copy(total_ref.at[part], out_hbm.at[:, columns], out_sem.at[part])
+
+    def pass_on(i):
+        given, part = turn(i)
+
+        @pl.when(given)
+        def _():
+            give_copy(part).start()
+
+        @pl.when(jnp.logical_not(given))
+        def _():
+            out_copy(part).start()
+
+    def project(i, _):
+        given, part = turn(i)
+        first_slab = slabs * (part + parts * jnp.where(given, 1 - core, core))
+
+        @pl.when(i == 2 * parts - 1)
+        def _():
+            arrived_at(far)
+
+        weight = jnp.concatenate([wbuf[first_slab + j] for j in range(slabs)], axis=1)
+        product = jnp.dot(att_ref[...], weight, preferred_element_type=jnp.float32)
+
+        @pl.when(i > 0)
+        def _():
+            pass_on(i - 1)
+
+        @pl.when(given)
+        def _():
+            give_ref[part] = product.astype(jnp.bfloat16)
+
+        @pl.when(jnp.logical_not(given))
+        def _():
+            give_copy(part).wait_recv()
+            total_ref[part] = (product + take_ref[part].astype(jnp.float32)).astype(jnp.bfloat16)
+
         return 0
 
-    lax.fori_loop(1, n, arrived, 0)
-
-    pairs = n // 4
-
-    def product(pair):
-        weight = jnp.concatenate([wbuf[2 * pair], wbuf[2 * pair + 1]], axis=1)
-        return jnp.dot(att_ref[...], weight, preferred_element_type=jnp.float32)
-
-    def give_copy(i):
-        return pltpu.make_async_remote_copy(
-            src_ref=give_ref.at[i], dst_ref=take_ref.at[i], send_sem=give_send.at[i], recv_sem=take_recv.at[i],
-            device_id=to_twin, device_id_type=MESH,
-        )
-
-    def give(i, _):
-        give_ref[i] = product((1 - core) * pairs + i).astype(jnp.bfloat16)
-
-        @pl.when(i > 0)
-        def _():
-            give_copy(i - 1).start()
-
-        return 0
-
-    lax.fori_loop(0, pairs, give, 0)
-    give_copy(pairs - 1).start()
-
-    def keep(i, _):
-        total = product(core * pairs + i)
-        give_copy(i).wait_recv()
-        columns = pl.ds(pl.multiple_of(i * give_ref.shape[2], give_ref.shape[2]), give_ref.shape[2])
-        out_ref[:, columns] = (total + take_ref[i].astype(jnp.float32)).astype(jnp.bfloat16)
-        return 0
-
-    lax.fori_loop(0, pairs, keep, 0)
-
-    def sent(s, _):
-        a, b = behind(s), ahead(s)
-        k_copy(0, a).wait_send()
-        v_copy(1, b).wait_send()
-
-        @pl.when(s < steps - 1)
-        def _():
-            k_copy(1, b).wait_send()
-            v_copy(0, a).wait_send()
-            w_copy(0, a).wait_send()
-            w_copy(1, b).wait_send()
-
-        @pl.when(s == steps - 1)
-        def _():
-            w_last_copy(0, a).wait_send()
-            w_last_copy(1, b).wait_send()
-
-        return 0
-
-    lax.fori_loop(1, steps, sent, 0)
+    lax.fori_loop(0, 2 * parts, project, 0)
+    pass_on(2 * parts - 1)
+
+    each(steps - 3, steps, sent)
+    sent_aside(far)
     for d in (0, 1):
         for copy in (k_copy, v_copy, w_copy):
             copy(d, me).wait_send()
-
-    def passed(s, _):
-        slot = ahead(s)
-        x_copy(slot, mine).wait_send()
-        y_copy(slot, mine).wait_send()
-        yd_copy(slot, of_x).wait_send()
-        xd_copy(slot, of_y).wait_send()
-        return 0
-
-    lax.fori_loop(1, n, passed, 0)
-
-    def given(i, _):
-        give_copy(i).wait_send()
-        return 0
-
-    lax.fori_loop(0, pairs, given, 0)
+    for part in range(parts):
+        give_copy(part).wait_send()
+        out_copy(part).wait()
 
 
 def local(n, row_stride, query_states, key_states, value_rows, positions, out_weight):
@@ -371,7 +423,8 @@
     heads = query_heads // kv_heads
     half = tokens // 2
     rows, slab = out_weight.shape
-    pairs = n // 4
+    parts = max(n // (2 * SLABS), 1)
+    slabs = n // (2 * parts)
     width = heads * half
     dma, bf16, f32 = pltpu.SemaphoreType.DMA, jnp.bfloat16, jnp.float32
     anywhere = pl.BlockSpec(memory_space=pl.ANY)
@@ -379,7 +432,7 @@
         functools.partial(kernel, n, row_stride, kv_heads, half),
         out_shape=jax.ShapeDtypeStruct((tokens, n // 2 * slab), bf16),
         in_specs=[anywhere] * 5,
-        out_specs=pl.BlockSpec(memory_space=pltpu.VMEM),
+        out_specs=anywhere,
         scratch_shapes=[
             pltpu.VMEM(query_states.shape, bf16),
             pltpu.VMEM(key_states.shape, bf16),
@@ -393,8 +446,9 @@
             pltpu.VMEM((kv_heads, 2, 1, width), f32),
             pltpu.VMEM((kv_heads, 2, 1, width), f32),
             pltpu.VMEM((tokens, query_heads * head_size), bf16),
-            pltpu.VMEM((pairs, tokens, 2 * slab), bf16),
-            pltpu.VMEM((pairs, tokens, 2 * slab), bf16),
+            pltpu.VMEM((parts, tokens, slabs * slab), bf16),
+            pltpu.VMEM((parts, tokens, slabs * slab), bf16),
+            pltpu.VMEM((parts, tokens, slabs * slab), bf16),
             dma((5,)),
             dma((2, n)),
             dma((2, n)),
@@ -411,8 +465,9 @@
             dma((n,)),
             dma((n,)),
             dma((n,)),
-            dma((pairs,)),
-            dma((pairs,)),
+            dma((parts,)),
+            dma((parts,)),
+            dma((parts,)),
         ],
         compiler_params=pltpu.CompilerParams(
             collective_id=0, has_side_effects=True, vmem_limit_bytes=62 * 1024 * 1024

time: 183 us -> 180 us (0.984)
  Pallas kernels: 181 us -> 178 us
    pallas_call x1, Pallas kernels: 181 us -> 178 us  [local(): pl.pallas_call(functools.partial(kernel, n, row_stride, kv_heads, half),...]
where the time goes in v3:
time: 180 us
  Pallas kernels  178 us (99%)
  local copies, waits for them, and re-layouts  2.3 us (1%)
    pallas_call x1, Pallas kernels, local(): pl.pallas_call(functools.partial(kernel, n, row_stride, kv_heads, half),...  178 us

profile of v3, /device:TPU:37, one launch (start us, length us, event | category | flops | bytes accessed | tf_op | source)
XLA Modules:
  0.0 180.4 jit_solution(16576063709065557925)
XLA Ops:
  0.0 178.0 %shard_map.55 = bf16[256,2048]{1,0:T(8,128)(2,1)} custom-call(bf16[256,16,128]{2,1,0:T(8,128)(2,1)} %q_hbm.1, bf16[256,2,128]{2,1,0:T(2,128)(2,1)} %k_hbm.1, bf16[256,2,128]{2,1,0:T(2,128)(2,1)} %v_hbm.1, s32[2,128]{1,0:T(2,128)} %bitcast.1, bf16[2048,128]{1,0:T(8,128)(2,1)} %w_hbm.1), custom_call_target="tpu_custom_call" | custom-call | tf_op jit(solution)/shard_map/pallas_call | solution.py:431
  178.1 2.3 %copy.7 = bf16[256,2048]{1,0:T(8,128)(2,1)} copy(bf16[256,2048]{1,0:T(8,128)(2,1)} %shard_map.55) | data formatting | bytes 2097152

commit v4 on v3

--- a/solution.py
+++ b/solution.py
@@ -280,11 +280,6 @@
 
         @pl.when(s > 1)
         def _():
-            relay(behind(s - 1))
-            relay(ahead(s - 1))
-
-        @pl.when(s > 1)
-        def _():
             attend(ahead(s - 1), 0)
 
         k_copy(0, a).wait_recv()
@@ -297,6 +292,8 @@
 
         @pl.when(s > 1)
         def _():
+            relay(behind(s - 1))
+            relay(ahead(s - 1))
             attend(ahead(s - 1), 1)
 
         v_copy(0, a).wait_recv()
@@ -325,9 +322,9 @@
     w_last_copy(0, far).wait_recv()
     w_last_copy(1, far).wait_recv()
     side(far)
+    attend_all(ahead(steps - 1))
     relay(behind(steps - 1))
     relay(ahead(steps - 1))
-    attend_all(ahead(steps - 1))
     k_copy(0, far).wait_recv()
     v_copy(1, far).wait_recv()
     attend_all(far)

time: 180 us -> 180 us (level)
  no operation moved by 1% of the time
where the time goes in v4:
time: 180 us
  Pallas kernels  178 us (99%)
  local copies, waits for them, and re-layouts  2.3 us (1%)
    pallas_call x1, Pallas kernels, local(): pl.pallas_call(functools.partial(kernel, n, row_stride, kv_heads, half),...  178 us

profile of v4, /device:TPU:37, one launch (start us, length us, event | category | flops | bytes accessed | tf_op | source)
XLA Modules:
  0.0 180.4 jit_solution(1651363763243563138)
XLA Ops:
  0.0 178.0 %shard_map.55 = bf16[256,2048]{1,0:T(8,128)(2,1)} custom-call(bf16[256,16,128]{2,1,0:T(8,128)(2,1)} %q_hbm.1, bf16[256,2,128]{2,1,0:T(2,128)(2,1)} %k_hbm.1, bf16[256,2,128]{2,1,0:T(2,128)(2,1)} %v_hbm.1, s32[2,128]{1,0:T(2,128)} %bitcast.1, bf16[2048,128]{1,0:T(8,128)(2,1)} %w_hbm.1), custom_call_target="tpu_custom_call" | custom-call | tf_op jit(solution)/shard_map/pallas_call | solution.py:428
  178.1 2.3 %copy.7 = bf16[256,2048]{1,0:T(8,128)(2,1)} copy(bf16[256,2048]{1,0:T(8,128)(2,1)} %shard_map.55) | data formatting | bytes 2097152
